TPU v7x, 32 devices: a whole 2x2x4 slice. The times are simulated.
32 devices in a mesh: rows: 8 (over z, y), cols: 4 (over x, core).
Axes of the slice: x: 2, y: 2, z: 4, core: 2. Of those that a mesh axis runs over, the one named last changes fastest.
Arguments:
- points: bfloat16 [4096, 256], P(('rows', 'cols')), may hold values from -6 to 6
- start_vectors: float32 [8, 4096], P(None, ('rows', 'cols')), may hold values from -6 to 6
- degree: bfloat16 [4096], P(('rows', 'cols')), may hold values from 0.19921875 to 2
Outputs:
- embedding: float32 [8, 4096], P(None, ('rows', 'cols'))
All inputs are finite; a program needn't handle non-finite values.
Results may differ from a plain program's by a relative error of at most 0.0034.
Values may be sent and summed in bfloat16 or wider, within the bound.
A program may use at most 64 MiB of HBM per device.

v0:
```python
import jax
import jax.numpy as jnp
from jax import lax
from jax.sharding import PartitionSpec as P

ITERS = 3


def body(points, start_vectors, degree):
    row_count = lax.axis_size("rows")
    col_count = lax.axis_size("cols")
    row_place = lax.axis_index("rows")
    col_place = lax.axis_index("cols")
    span_size = points.shape[0]
    sharpness = 4.0 / points.shape[1]
    row_points, row_degree = (
        lax.all_gather(points, "cols", axis=0, tiled=True),
        lax.all_gather(degree, "cols", axis=0, tiled=True),
    )
    row_total = row_points.shape[0]
    row_float = row_points.astype(jnp.float32)
    row_norms = jnp.sum(row_float * row_float, axis=1)
    row_slots = jnp.arange(row_total, dtype=jnp.int32)
    row_global = (
        row_place * col_count + row_slots // span_size
    ) * span_size + row_slots % span_size

    def kernel_block(x_block, col_norms, first_slot):
        inner = lax.dot_general(
            row_points, x_block, (((1,), (1,)), ((), ())), preferred_element_type=jnp.float32
        )
        distance = row_norms[:, None] + col_norms[None, :] - 2.0 * inner
        kernel = jnp.exp(-sharpness * distance)
        col_slots = first_slot + jnp.arange(x_block.shape[0], dtype=jnp.int32)
        col_global = (
            col_slots // span_size * col_count + col_place
        ) * span_size + col_slots % span_size
        return jnp.where(
            row_global[:, None] == col_global[None, :], jnp.float32(0.0), kernel
        ).astype(jnp.bfloat16)

    vectors = start_vectors
    for iteration in range(ITERS):
        empty = jnp.zeros((vectors.shape[0], row_total), jnp.float32)
        sending = vectors.T.astype(jnp.bfloat16)
        x_piece = lax.all_gather(points, "rows", axis=0, tiled=True)
        v_piece = lax.all_gather(sending, "rows", axis=0, tiled=True)
        piece_rows = x_piece.shape[0]
        block_size = 512
        block_count = piece_rows // block_size

        def accumulate(block_index, running):
            offset = block_index * block_size
            x_block = lax.dynamic_slice_in_dim(x_piece, offset, block_size, 0)
            v_block = lax.dynamic_slice_in_dim(v_piece, offset, block_size, 0)
            x_float = x_block.astype(jnp.float32)
            col_norms = jnp.sum(x_float * x_float, axis=1)
            kernel = kernel_block(x_block, col_norms, offset)
            return running + lax.dot_general(
                v_block, kernel, (((0,), (1,)), ((), ())), preferred_element_type=jnp.float32
            )

        partial_value = lax.fori_loop(0, block_count, accumulate, empty)
        summed = lax.psum(partial_value, "cols")
        row_state = summed / row_degree.astype(jnp.float32)[None, :]
        vectors = lax.dynamic_slice_in_dim(row_state, col_place * span_size, span_size, 1)
    magnitude = lax.psum(jnp.sum(jnp.abs(row_state), axis=1), "rows")
    mean_abs = magnitude / (span_size * row_count * col_count)
    return vectors / (mean_abs[:, None] + 1e-06)


def solution(mesh):
    return jax.shard_map(
        body,
        mesh=mesh,
        in_specs=(P(("rows", "cols"), None), P(None, ("rows", "cols")), P(("rows", "cols"))),
        out_specs=P(None, ("rows", "cols")),
        check_vma=False,
    )
```

profile of v0, /device:TPU:0, one launch (start us, length us, event | category | flops | bytes accessed | tf_op | source)
XLA Modules:
  0.0 177.6 jit_solution(2372064318550203494)
XLA Ops:
  0.0 0.0 copy-start.2
  0.0 0.7 copy-done.2
  0.7 6.0 %all-gather = bf16[4,1,128]{2,1,0:T(2,128)(2,1)S(1)} all-gather(bf16[1,1,128]{2,1,0:T(2,128)(2,1)S(1)} %bitcast.73), channel_id=1, replica_groups=mesh['rows'=8,'cols'=4] {'cols'}, dimensions={0}, use_global_device_ids=true | all-gather | bytes 1280 | tf_op jit(solution)/shard_map/all_gather | solution.py:18
  6.7 0.1 dynamic-slice
  6.7 6.5 %all_gather.21 = bf16[512,256]{1,0:T(8,128)(2,1)S(1)} all-gather(bf16[128,256]{1,0:T(8,128)(2,1)} %param.9), channel_id=1, replica_groups=mesh['rows'=8,'cols'=4] {'cols'}, dimensions={0}, use_global_device_ids=true | all-gather | bytes 327680 | tf_op jit(solution)/shard_map/all_gather | solution.py:17
  13.2 0.0 copy-start
  13.2 0.1 multiply_reduce_fusion.3
  13.4 0.7 copy-done
  14.0 0.0 copy-start.1
  14.0 32.1 %all_gather.22 = bf16[1024,256]{1,0:T(8,128)(2,1)S(1)} all-gather(bf16[128,256]{1,0:T(8,128)(2,1)S(1)} %copy-done), channel_id=1, replica_groups=mesh['rows'=8,'cols'=4] {'rows'}, dimensions={0}, use_global_device_ids=true | all-gather | bytes 589824 | tf_op jit(solution)/shard_map/all_gather | solution.py:46
  46.2 0.0 copy-done.1
  46.2 26.1 %all_gather.20 = bf16[1024,8]{0,1:T(8,128)(2,1)S(1)} all-gather(bf16[128,8]{0,1:T(8,128)(2,1)S(1)} %convert_bitcast_fusion), channel_id=1, replica_groups=mesh['rows'=8,'cols'=4] {'rows'}, dimensions={0}, use_global_device_ids=true | all-gather | bytes 18432 | tf_op jit(solution)/shard_map/all_gather | solution.py:47
  72.3 1.6 while.48
  72.3 0.1 multiply_reduce_fusion.7
  72.5 0.6 fusion.155
  73.1 0.2 multiply_reduce_fusion.7
  73.3 0.6 fusion.155
  73.9 10.1 %psum.28 = f32[8,512]{1,0:T(8,128)S(1)} all-reduce(f32[8,512]{1,0:T(8,128)S(1)} %get-tuple-element.608), channel_id=1, replica_groups=mesh['rows'=8,'cols'=4] {'cols'}, use_global_device_ids=true, to_apply=%region_4.5 | all-reduce | flops 4096 | bytes 32768 | tf_op jit(solution)/shard_map/psum | solution.py:64
  84.0 26.1 %all_gather.24 = bf16[1024,8]{0,1:T(8,128)(2,1)S(1)} all-gather(bf16[128,8]{0,1:T(8,128)(2,1)S(1)} %fusion.131), channel_id=1, replica_groups=mesh['rows'=8,'cols'=4] {'rows'}, dimensions={0}, use_global_device_ids=true | all-gather | bytes 18432 | tf_op jit(solution)/shard_map/all_gather | solution.py:47
  110.1 1.6 while.49
  110.1 0.1 multiply_reduce_fusion.8
  110.3 0.6 fusion.160
  110.9 0.2 multiply_reduce_fusion.8
  111.1 0.6 fusion.160
  111.7 10.1 %psum.29 = f32[8,512]{1,0:T(8,128)S(1)} all-reduce(f32[8,512]{1,0:T(8,128)S(1)} %get-tuple-element.609), channel_id=1, replica_groups=mesh['rows'=8,'cols'=4] {'cols'}, use_global_device_ids=true, to_apply=%region_8.9 | all-reduce | flops 4096 | bytes 32768 | tf_op jit(solution)/shard_map/psum | solution.py:64
  121.8 26.1 %all_gather.25 = bf16[1024,8]{0,1:T(8,128)(2,1)S(1)} all-gather(bf16[128,8]{0,1:T(8,128)(2,1)S(1)} %fusion.132), channel_id=1, replica_groups=mesh['rows'=8,'cols'=4] {'rows'}, dimensions={0}, use_global_device_ids=true | all-gather | bytes 18432 | tf_op jit(solution)/shard_map/all_gather | solution.py:47
  148.0 1.6 while.50
  148.0 0.1 multiply_reduce_fusion.9
  148.1 0.6 fusion.165
  148.7 0.2 multiply_reduce_fusion.9
  148.9 0.6 fusion.165
  149.5 10.1 %psum.30 = f32[8,512]{1,0:T(8,128)S(1)} all-reduce(f32[8,512]{1,0:T(8,128)S(1)} %get-tuple-element.610), channel_id=1, replica_groups=mesh['rows'=8,'cols'=4] {'cols'}, use_global_device_ids=true, to_apply=%region_12.13 | all-reduce | flops 4096 | bytes 32768 | tf_op jit(solution)/shard_map/psum | solution.py:64
  159.7 0.1 abs_reduce_fusion
  159.8 17.1 %psum.31 = f32[8]{0:T(128)S(1)} all-reduce(f32[8]{0:T(128)S(1)} %get-tuple-element.749), channel_id=1, replica_groups=mesh['rows'=8,'cols'=4] {'rows'}, use_global_device_ids=true, to_apply=%region_14.15 | all-reduce | flops 8 | bytes 64 | tf_op jit(solution)/shard_map/psum | solution.py:67
  176.9 0.7 dynamic-slice_divide_fusion.2
  (14 shorter events, 0.1 us)
Async XLA Ops:
  0.0 0.7 copy-start.2
  13.2 0.8 copy-start
  14.0 32.1 %copy-start.1 = (f32[8,128]{1,0:T(8,128)S(1)}, f32[8,128]{1,0:T(8,128)}, u32[]{:S(2)}) copy-start(f32[8,128]{1,0:T(8,128)} %param.10) | copy-start | bytes 12292
where the time goes:
time: 178 us
  blocking collectives  170 us (96%)
  matrix products  3.57 us (2%)
  other arithmetic  2.03 us (1%)
    all_gather x3, blocking collectives, body(): v_piece = lax.all_gather(sending, 'rows', axis=0, tiled=True)  78.3 us
    all_gather x1, blocking collectives, body(): x_piece = lax.all_gather(points, 'rows', axis=0, tiled=True)  32.1 us
    psum x3, blocking collectives, body(): summed = lax.psum(partial_value, 'cols')  30.4 us
    psum x1, blocking collectives, body(): magnitude = lax.psum(jnp.sum(jnp.abs(row_state), axis=1), 'rows')  17.1 us
    all_gather x1, blocking collectives, body(): lax.all_gather(points, 'cols', axis=0, tiled=True)  6.47 us
    all_gather x1, blocking collectives, body(): lax.all_gather(degree, 'cols', axis=0, tiled=True)  5.99 us
    dot_general x6, matrix products, accumulate(): lax.dot_general(v_block, kernel, (((0,), (1,)), ((), ())), preferred_elem...  3.57 us

commit v1 on v0

v1 whole, which is shorter than its diff:
```python
import functools
import math

import jax
import jax.numpy as jnp
from jax import lax
from jax.experimental import pallas as pl
from jax.experimental.pallas import tpu as pltpu
from jax.sharding import PartitionSpec as P

ITERS = 3
MESH = pl.DeviceIdType.MESH
F32, BF16 = jnp.float32, jnp.bfloat16
NT = (((1,), (1,)), ((), ()))
NN = (((1,), (0,)), ((), ()))


def kernel(
    na, nb, nc, x_ref, v_ref, d_ref, o_ref,
    xr, xc, v0, vb, rs, pt, mg, at, hj,
    xr_s, xr_r, xc_s, xc_r, v0_s, v0_r, vb_s, vb_r, rs_s, rs_r, mg_s, mg_r,
):
    span, feats = x_ref.shape
    nq, nd = na // 2, na * nb
    sharp = 4.0 / feats * math.log2(math.e)
    flat = lax.axis_index("rows") * nc + lax.axis_index("cols")
    b, a = flat // na, flat % na
    q, p = a // 2, a % 2

    def device(flat_index):
        return (flat_index // nc, flat_index % nc)

    def member(chip, parity):
        return device(b * na + chip * 2 + parity)

    def line(step):
        return device((b + step + nb) % nb * na + a)

    pending = []

    def send(src, dst, send_sem, recv_sem, target):
        copy = pltpu.make_async_remote_copy(
            src_ref=src, dst_ref=dst, send_sem=send_sem, recv_sem=recv_sem,
            device_id=target, device_id_type=MESH,
        )
        copy.start()
        pending.append(copy)
        return copy

    barrier = pltpu.get_barrier_semaphore()
    for step in range(na):
        if step:
            peer = device(b * na + (a + step) % na)
            pl.semaphore_signal(barrier, inc=1, device_id=peer, device_id_type=MESH)
    for step in range(1, nb):
        pl.semaphore_signal(barrier, inc=1, device_id=line(step), device_id_type=MESH)
    pl.semaphore_wait(barrier, na + nb - 2)

    partner = member(q, 1 - p)
    xr_in, xc_in, v0_in = {}, {}, {}
    for kq in range(1, nq):
        slot = 2 * kq
        xr_in[slot] = send(
            x_ref, xr.at[slot], xr_s.at[slot], xr_r.at[slot], member((q + kq) % nq, p)
        )
    for kb in range(1, nb):
        xc_in[kb] = send(x_ref, xc.at[kb], xc_s.at[kb], xc_r.at[kb], line(kb))
    for kb in range(1, nb):
        v0_in[kb] = send(v_ref, v0.at[kb], v0_s.at[kb], v0_r.at[kb], line(kb))
    xr_in[1] = send(x_ref, xr.at[1], xr_s.at[1], xr_r.at[1], partner)

    def squares(x):
        xf = x.astype(F32)
        sq = xf * xf
        high = sq.astype(BF16)
        return high, (sq - high.astype(F32)).astype(BF16)

    wide = jnp.ones((feats, 128), BF16)
    thin = jnp.ones((8, feats), BF16)

    def dot(l, r, dims):
        return lax.dot_general(l, r, dims, preferred_element_type=F32)

    def store_norm(kb, x):
        high, low = squares(x)
        hj[kb] = sharp * (dot(high, wide, NN) + dot(low, wide, NN))

    def row_norm(x):
        high, low = squares(x)
        return (sharp * (dot(thin, high, NT) + dot(thin, low, NT)))[0:1, :]

    def unit(kb, kq, xj, xi, hi, diagonal=False):
        g = dot(xj, xi, NT)
        hcol = hj[kb]
        for half in range(2):
            lanes = slice(half * span, (half + 1) * span)
            e = jnp.exp2((2.0 * sharp) * g[:, lanes] - (hcol + hi[:, lanes]))
            if diagonal and half == 0:
                rows = lax.broadcasted_iota(jnp.int32, (span, span), 0)
                cols = lax.broadcasted_iota(jnp.int32, (span, span), 1)
                e = jnp.where(rows == cols, 0.0, e)
            at[kb, :, (2 * kq + half) * span:(2 * kq + half + 1) * span] = e.astype(BF16)

    def others(body):
        if nb <= 4:
            for kb in range(1, nb):
                body(kb)
        else:
            def looped(kb, carry):
                body(kb)
                return carry
            lax.fori_loop(1, nb, looped, 0)

    own = x_ref[...]
    store_norm(0, own)
    xr_in[1].wait_recv()
    xi = jnp.concatenate([own, xr[1]], axis=0)
    hi0 = row_norm(xi)
    unit(0, 0, own, xi, hi0, diagonal=True)

    for kq in range(1, nq):
        slot = 2 * kq
        xr_in[slot].wait_recv()
        xr_in[slot + 1] = send(
            xr.at[slot], xr.at[slot + 1], xr_s.at[slot + 1], xr_r.at[slot + 1], partner
        )
    for kb in range(1, nb):
        xc_in[kb].wait_recv()

    def first(kb):
        xj = xc[kb]
        store_norm(kb, xj)
        unit(kb, 0, xj, xi, hi0)

    others(first)
    for kq in range(1, nq):
        xr_in[2 * kq + 1].wait_recv()
        pair = jnp.concatenate([xr[2 * kq], xr[2 * kq + 1]], axis=0)
        hi = row_norm(pair)
        unit(0, kq, own, pair, hi)

        def more(kb, kq=kq, pair=pair, hi=hi):
            unit(kb, kq, xc[kb], pair, hi)

        others(more)

    for kb in range(1, nb):
        v0_in[kb].wait_recv()
    v_parts = [v_ref[...].astype(BF16)] + [v0[kb].astype(BF16) for kb in range(1, nb)]
    inv = d_ref[...].astype(F32)

    for it in range(ITERS):
        product = jnp.zeros((v_ref.shape[0], na * span), F32)
        for kb in range(nb):
            product = product + dot(v_parts[kb], at[kb], NN)
        rs_in = {}
        for slot in range(1, na):
            pt[it, slot] = product[:, slot * span:(slot + 1) * span]
        for slot in range(1, na):
            kq, kp = slot // 2, slot % 2
            parity = p if kp == 0 else 1 - p
            rs_in[slot] = send(
                pt.at[it, slot], rs.at[it, slot], rs_s.at[it, slot], rs_r.at[it, slot],
                member((q - kq + nq) % nq, parity),
            )
        total = product[:, :span]
        for slot in range(1, na):
            rs_in[slot].wait_recv()
            total = total + rs[it, slot]
        mine = total / inv
        if it < ITERS - 1:
            sending = mine.astype(BF16)
            vb[it, 0] = sending
            vb_in = {}
            for kb in range(1, nb):
                vb_in[kb] = send(
                    vb.at[it, 0], vb.at[it, kb], vb_s.at[it, kb], vb_r.at[it, kb], line(kb)
                )
            v_parts = [sending]
            for kb in range(1, nb):
                vb_in[kb].wait_recv()
                v_parts.append(vb[it, kb])

    nk = v_ref.shape[0]
    sums = jnp.sum(jnp.abs(mine), axis=1, keepdims=True)
    eye = lax.broadcasted_iota(jnp.int32, (nk, 128), 0) == lax.broadcasted_iota(
        jnp.int32, (nk, 128), 1
    )
    mg[0] = jnp.sum(jnp.where(eye, sums, 0.0), axis=0, keepdims=True)

    def spread(step):
        return pltpu.make_async_remote_copy(
            src_ref=mg.at[0], dst_ref=mg.at[step], send_sem=mg_s.at[step],
            recv_sem=mg_r.at[step], device_id=device((flat + step) % nd),
            device_id_type=MESH,
        )

    def start_one(step, carry):
        spread(step).start()
        return carry

    def wait_one(step, carry):
        spread(step).wait_recv()
        return carry

    def done_one(step, carry):
        spread(step).wait_send()
        return carry

    lax.fori_loop(1, nd, start_one, 0)
    for copy in pending:
        copy.wait_send()
    lax.fori_loop(1, nd, wait_one, 0)
    every = jnp.sum(mg[...], axis=0)
    mean = jnp.sum(jnp.where(eye, every, 0.0), axis=1, keepdims=True) / (span * nd)
    o_ref[...] = mine / (mean + 1e-06)
    lax.fori_loop(1, nd, done_one, 0)


def solution(mesh):
    nr, nc = mesh.shape["rows"], mesh.shape["cols"]
    low = 1
    while low * nc < nr // low:
        low *= 2
    na, nb = low * nc, nr // low

    def body(points, start_vectors, degree):
        span, feats = points.shape
        nk = start_vectors.shape[0]
        dma = pltpu.SemaphoreType.DMA
        return pl.pallas_call(
            functools.partial(kernel, na, nb, nc),
            out_shape=jax.ShapeDtypeStruct((nk, span), F32),
            in_specs=[pl.BlockSpec(memory_space=pltpu.VMEM)] * 3,
            out_specs=pl.BlockSpec(memory_space=pltpu.VMEM),
            scratch_shapes=[
                pltpu.VMEM((na, span, feats), BF16),
                pltpu.VMEM((nb, span, feats), BF16),
                pltpu.VMEM((nb, nk, span), F32),
                pltpu.VMEM((ITERS - 1, nb, nk, span), BF16),
                pltpu.VMEM((ITERS, na, nk, span), F32),
                pltpu.VMEM((ITERS, na, nk, span), F32),
                pltpu.VMEM((na * nb, 1, 128), F32),
                pltpu.VMEM((nb, span, na * span), BF16),
                pltpu.VMEM((nb, span, 128), F32),
                dma((na,)), dma((na,)), dma((nb,)), dma((nb,)), dma((nb,)), dma((nb,)),
                dma((ITERS - 1, nb)), dma((ITERS - 1, nb)),
                dma((ITERS, na)), dma((ITERS, na)),
                dma((na * nb,)), dma((na * nb,)),
            ],
            compiler_params=pltpu.CompilerParams(collective_id=0, has_side_effects=True),
        )(points, start_vectors, degree.reshape(1, span))

    return jax.shard_map(
        body,
        mesh=mesh,
        in_specs=(P(("rows", "cols"), None), P(None, ("rows", "cols")), P(("rows", "cols"))),
        out_specs=P(None, ("rows", "cols")),
        check_vma=False,
    )
```

time: 178 us -> 40.9 us (0.23)
  blocking collectives: 170 us -> 0 us
  Pallas kernels: 0 us -> 39.4 us
  matrix products: 3.57 us -> 0 us
  other arithmetic: 2.03 us -> 0 us
    all_gather x6 -> x0, blocking collectives: 123 us -> none  [the longest x3 78.3 us: body(): v_piece = lax.all_gather(sending, 'rows', axis=0, tiled=True)]
    psum x4 -> x0, blocking collectives: 47.5 us -> none  [the longest x3 30.4 us: body(): summed = lax.psum(partial_value, 'cols')]
    pallas_call x0 -> x1, Pallas kernels: none -> 39.4 us  [body(): pl.pallas_call(functools.partial(kernel, na, nb, nc), out_shape=jax.Shape...]
    dot_general x6 -> x0, matrix products: 3.57 us -> none  [accumulate(): lax.dot_general(v_block, kernel, (((0,), (1,)), ((), ())), preferred_elem...]
where the time goes in v1:
time: 40.9 us; the launch traced here: 40.7 us
  Pallas kernels  39.4 us (96%)
  local copies, waits for them, and re-layouts  1.28 us (3%)
    pallas_call x1, Pallas kernels, body(): pl.pallas_call(functools.partial(kernel, na, nb, nc), out_shape=jax.Shape...  39.4 us
    unnamed x1, local copies, waits for them, and re-layouts  1.28 us

profile of v1, /device:TPU:0, one launch (start us, length us, event | category | flops | bytes accessed | tf_op | source)
XLA Modules:
  0.0 40.7 jit_solution(13234730400202751153)
XLA Ops:
  0.0 39.4 %shard_map.37 = f32[8,128]{1,0:T(8,128)} custom-call(bf16[128,256]{1,0:T(8,128)(2,1)} %x_ref.1, f32[8,128]{1,0:T(8,128)} %v_ref.1, bf16[1,128]{1,0:T(2,128)(2,1)} %bitcast.1), custom_call_target="tpu_custom_call" | custom-call | tf_op jit(solution)/shard_map/pallas_call | solution.py:231
  39.4 1.3 %copy.5 = f32[8,128]{1,0:T(8,128)} copy(f32[8,128]{1,0:T(8,128)} %shard_map.37) | data formatting | bytes 8192

commit v2 on v1

v2 whole, which is shorter than its diff:
```python
import functools
import math

import jax
import jax.numpy as jnp
from jax import lax
from jax.experimental import pallas as pl
from jax.experimental.pallas import tpu as pltpu
from jax.sharding import PartitionSpec as P

ITERS = 3
MESH = pl.DeviceIdType.MESH
F32, BF16 = jnp.float32, jnp.bfloat16
NT = (((1,), (1,)), ((), ()))
NN = (((1,), (0,)), ((), ()))


def kernel(
    na, nb, nc, x_hbm, v_hbm, d_hbm, o_ref,
    xr, xc, v0, db, da, zb, ab, mg, at, hj, d_ref, in_s,
    xr_s, xr_r, xc_s, xc_r, v0_s, v0_r, db_s, db_r, da_s, da_r,
    zb_s, zb_r, ab_s, ab_r, mg_s, mg_r,
):
    span, feats = x_hbm.shape
    nk = v_hbm.shape[0]
    nq, nd = na // 2, na * nb
    x_ref, v_ref = xr.at[0], v0.at[0]
    sharp = 4.0 / feats * math.log2(math.e)
    flat = lax.axis_index("rows") * nc + lax.axis_index("cols")
    b, a = flat // na, flat % na
    q, p = a // 2, a % 2

    def device(flat_index):
        return (flat_index // nc, flat_index % nc)

    def member(chip, parity):
        return device(b * na + chip * 2 + parity)

    def line(step):
        return device((b + step + nb) % nb * na + a)

    pending = []

    def send(src, dst, send_sem, recv_sem, target):
        copy = pltpu.make_async_remote_copy(
            src_ref=src, dst_ref=dst, send_sem=send_sem, recv_sem=recv_sem,
            device_id=target, device_id_type=MESH,
        )
        copy.start()
        pending.append(copy)
        return copy

    loads = [
        pltpu.make_async_copy(src, dst, in_s.at[i])
        for i, (src, dst) in enumerate([(x_hbm, x_ref), (v_hbm, v_ref), (d_hbm, d_ref)])
    ]
    for load in loads:
        load.start()

    barrier = pltpu.get_barrier_semaphore()
    for step in range(na):
        if step:
            peer = device(b * na + (a + step) % na)
            pl.semaphore_signal(barrier, inc=1, device_id=peer, device_id_type=MESH)
    for step in range(1, nb):
        pl.semaphore_signal(barrier, inc=1, device_id=line(step), device_id_type=MESH)
    loads[2].wait()
    degree = d_ref[...].astype(F32)
    db[0] = degree
    da[0] = degree
    loads[0].wait()
    loads[1].wait()
    pl.semaphore_wait(barrier, na + nb - 2)

    partner = member(q, 1 - p)

    def slot_member(slot):
        kq, kp = slot // 2, slot % 2
        return member((q + kq) % nq, p if kp == 0 else 1 - p)

    relay = nb == 4
    x_in, xc_in, v_in, db_in, da_in = {}, {}, {}, {}, {}

    def to_line(step):
        return pltpu.make_async_remote_copy(
            src_ref=x_ref, dst_ref=xc.at[step], send_sem=xc_s.at[step],
            recv_sem=xc_r.at[step], device_id=line(step), device_id_type=MESH,
        )

    order = [3, 1] if relay else list(range(1, nb))
    if relay:
        @pl.when(b % 3 == 0)
        def _():
            to_line(2).start()
    for kb in order:
        xc_in[kb] = send(x_ref, xc.at[kb], xc_s.at[kb], xc_r.at[kb], line(kb))
    for kq in range(1, nq):
        slot = 2 * kq
        x_in[slot] = send(x_ref, xr.at[slot], xr_s.at[slot], xr_r.at[slot], slot_member(slot))
    x_in[1] = send(x_ref, xr.at[1], xr_s.at[1], xr_r.at[1], partner)
    for kq in range(1, nq):
        slot = 2 * kq
        v_in[slot] = send(v_ref, v0.at[slot], v0_s.at[slot], v0_r.at[slot], slot_member(slot))
    v_in[1] = send(v_ref, v0.at[1], v0_s.at[1], v0_r.at[1], partner)
    for kb in range(1, nb):
        db_in[kb] = send(db.at[0], db.at[kb], db_s.at[kb], db_r.at[kb], line(kb))
    for slot in range(1, na):
        da_in[slot] = send(da.at[0], da.at[slot], da_s.at[slot], da_r.at[slot], slot_member(slot))

    def squares(x):
        xf = x.astype(F32)
        sq = xf * xf
        high = sq.astype(BF16)
        return high, (sq - high.astype(F32)).astype(BF16)

    wide = jnp.ones((feats, 128), BF16)
    thin = jnp.ones((8, feats), BF16)

    def dot(l, r, dims):
        return lax.dot_general(l, r, dims, preferred_element_type=F32)

    def store_norm(kb, x):
        high, low = squares(x)
        hj[kb] = sharp * (dot(high, wide, NN) + dot(low, wide, NN))

    def row_norm(x):
        high, low = squares(x)
        return (sharp * (dot(thin, high, NT) + dot(thin, low, NT)))[0:1, :]

    def unit(kb, kq, xj, xi, hi, diagonal=False):
        g = dot(xj, xi, NT)
        hcol = hj[kb]
        for half in range(2):
            lanes = slice(half * span, (half + 1) * span)
            e = jnp.exp2((2.0 * sharp) * g[:, lanes] - (hcol + hi[:, lanes]))
            if diagonal and half == 0:
                rows = lax.broadcasted_iota(jnp.int32, (span, span), 0)
                cols = lax.broadcasted_iota(jnp.int32, (span, span), 1)
                e = jnp.where(rows == cols, 0.0, e)
            at[kb, :, (2 * kq + half) * span:(2 * kq + half + 1) * span] = e.astype(BF16)

    def others(body):
        if nb <= 4:
            for kb in range(1, nb):
                body(kb)
        else:
            def looped(kb, carry):
                body(kb)
                return carry
            lax.fori_loop(1, nb, looped, 0)

    own = x_ref[...]
    store_norm(0, own)
    x_in[1].wait_recv()
    xi = jnp.concatenate([own, xr[1]], axis=0)
    hi0 = row_norm(xi)
    unit(0, 0, own, xi, hi0, diagonal=True)

    def pass_on(slot):
        x_in[slot].wait_recv()
        x_in[slot + 1] = send(
            xr.at[slot], xr.at[slot + 1], xr_s.at[slot + 1], xr_r.at[slot + 1], partner
        )

    def first(kb):
        xj = xc[kb]
        store_norm(kb, xj)
        unit(kb, 0, xj, xi, hi0)

    if relay:
        xc_in[1].wait_recv()
        xc_in[3].wait_recv()

        @pl.when(b % 3 != 0)
        def _():
            pltpu.make_async_remote_copy(
                src_ref=xc.at[(5 - 2 * b) % 4], dst_ref=xc.at[2], send_sem=xc_s.at[2],
                recv_sem=xc_r.at[2], device_id=line(2 * b - 3), device_id_type=MESH,
            ).start()
    for kq in range(1, nq):
        pass_on(2 * kq)
    for kq in range(1, nq):
        slot = 2 * kq
        v_in[slot].wait_recv()
        v_in[slot + 1] = send(
            v0.at[slot], v0.at[slot + 1], v0_s.at[slot + 1], v0_r.at[slot + 1], partner
        )
    if relay:
        first(1)
        first(3)
    his, pairs = [hi0], [xi]
    for kq in range(1, nq):
        x_in[2 * kq + 1].wait_recv()
        pairs.append(jnp.concatenate([xr[2 * kq], xr[2 * kq + 1]], axis=0))
        his.append(row_norm(pairs[kq]))
        unit(0, kq, own, pairs[kq], his[kq])
        if relay:
            unit(1, kq, xc[1], pairs[kq], his[kq])
            unit(3, kq, xc[3], pairs[kq], his[kq])
    if relay:
        to_line(2).wait_recv()
    else:
        for kb in range(1, nb):
            xc_in[kb].wait_recv()

    def rest(kb):
        first(kb)
        for kq in range(1, nq):
            unit(kb, kq, xc[kb], pairs[kq], his[kq])

    if relay:
        rest(2)
    else:
        others(rest)

    for slot in range(1, na):
        if slot % 2:
            v_in[slot].wait_recv()
        da_in[slot].wait_recv()
    for kb in range(1, nb):
        db_in[kb].wait_recv()
    col_degree = [db[kb] for kb in range(nb)]
    row_degree = [da[slot] for slot in range(na)]

    def to_columns(turn, row_vectors):
        wide_rows = jnp.concatenate(row_vectors, axis=1)
        part = [dot(wide_rows, at[kb], NT) for kb in range(nb)]
        for kb in range(nb):
            zb[turn, 0, :, kb * span:(kb + 1) * span] = part[kb]
        arriving = {
            kb: send(
                zb.at[turn, 0], zb.at[turn, kb], zb_s.at[turn, kb], zb_r.at[turn, kb], line(kb)
            )
            for kb in list(range(2, nb)) + [1]
        }
        for step in range(1, nb):
            arriving[step].wait_recv()
            for kb in range(nb):
                there = (kb - step) % nb
                part[kb] = part[kb] + zb[turn, step, :, there * span:(there + 1) * span]
        return [part[kb] / col_degree[kb] for kb in range(nb)]

    def to_rows(col_vectors):
        part = dot(col_vectors[0], at[0], NN)
        for kb in range(1, nb):
            part = part + dot(col_vectors[kb], at[kb], NN)
        ab[0] = part
        arriving = {
            slot: send(ab.at[0], ab.at[slot], ab_s.at[slot], ab_r.at[slot], slot_member(slot))
            for slot in list(range(2, na)) + [1]
        }
        part = [part[:, slot * span:(slot + 1) * span] for slot in range(na)]
        for step in [1] + list(range(2, na)):
            arriving[step].wait_recv()
            for slot in range(na):
                there = (slot // 2 - step // 2) % nq * 2 + (slot % 2 + step % 2) % 2
                part[slot] = part[slot] + ab[step, :, there * span:(there + 1) * span]
        return [part[slot] / row_degree[slot] for slot in range(na)]

    def rounded(vectors):
        return [piece.astype(BF16) for piece in vectors]

    vectors, on_rows, turn = [v0[slot] for slot in range(na)], True, 0
    for it in range(ITERS):
        if on_rows:
            vectors = to_columns(turn, rounded(vectors))
            turn += 1
        else:
            vectors = to_rows(rounded(vectors))
        on_rows = not on_rows
    mine = vectors[0]

    held = jnp.abs(mine)
    for kb in range(1, nb):
        held = held + jnp.abs(vectors[kb])
    sums = jnp.sum(held, axis=1, keepdims=True)
    eye = lax.broadcasted_iota(jnp.int32, (nk, 128), 0) == lax.broadcasted_iota(
        jnp.int32, (nk, 128), 1
    )
    mg[0] = jnp.sum(jnp.where(eye, sums, 0.0), axis=0, keepdims=True)

    mg_in = {
        slot: send(mg.at[0], mg.at[slot], mg_s.at[slot], mg_r.at[slot], slot_member(slot))
        for slot in list(range(2, na)) + [1]
    }
    for copy in pending[:-(na - 1)]:
        copy.wait_send()
    if relay:
        to_line(2).wait_send()
    for slot in range(1, na):
        mg_in[slot].wait_recv()
    every = jnp.sum(mg[...], axis=0)
    mean = jnp.sum(jnp.where(eye, every, 0.0), axis=1, keepdims=True) / (span * nd)
    o_ref[...] = mine / (mean + 1e-06)
    for slot in range(1, na):
        mg_in[slot].wait_send()


def solution(mesh):
    nr, nc = mesh.shape["rows"], mesh.shape["cols"]
    low = 1
    while low * nc < nr // low:
        low *= 2
    na, nb = low * nc, nr // low

    def body(points, start_vectors, degree):
        span, feats = points.shape
        nk = start_vectors.shape[0]
        dma = pltpu.SemaphoreType.DMA
        turns = (ITERS + 1) // 2
        return pl.pallas_call(
            functools.partial(kernel, na, nb, nc),
            out_shape=jax.ShapeDtypeStruct((nk, span), F32),
            in_specs=[pl.BlockSpec(memory_space=pl.ANY)] * 3,
            out_specs=pl.BlockSpec(memory_space=pltpu.VMEM),
            scratch_shapes=[
                pltpu.VMEM((na, span, feats), BF16),
                pltpu.VMEM((nb, span, feats), BF16),
                pltpu.VMEM((na, nk, span), F32),
                pltpu.VMEM((nb, 1, span), F32),
                pltpu.VMEM((na, 1, span), F32),
                pltpu.VMEM((turns, nb, nk, nb * span), F32),
                pltpu.VMEM((na, nk, na * span), F32),
                pltpu.VMEM((na, 1, 128), F32),
                pltpu.VMEM((nb, span, na * span), BF16),
                pltpu.VMEM((nb, span, 128), F32),
                pltpu.VMEM((1, span), BF16),
                dma((3,)),
                dma((na,)), dma((na,)), dma((nb,)), dma((nb,)), dma((na,)), dma((na,)),
                dma((nb,)), dma((nb,)), dma((na,)), dma((na,)),
                dma((turns, nb)), dma((turns, nb)), dma((na,)), dma((na,)),
                dma((na,)), dma((na,)),
            ],
            compiler_params=pltpu.CompilerParams(collective_id=0, has_side_effects=True),
        )(points, start_vectors, degree.reshape(1, span))

    return jax.shard_map(
        body,
        mesh=mesh,
        in_specs=(P(("rows", "cols"), None), P(None, ("rows", "cols")), P(("rows", "cols"))),
        out_specs=P(None, ("rows", "cols")),
        check_vma=False,
    )
```

time: 40.9 us -> 34.9 us (0.85)
  Pallas kernels: 39.4 us -> 33.4 us
    pallas_call x1, Pallas kernels: 39.4 us -> 33.4 us  [body(): pl.pallas_call(functools.partial(kernel, na, nb, nc), out_shape=jax.Shape...]
where the time goes in v2:
time: 34.9 us; the launch traced here: 34.7 us
  Pallas kernels  33.4 us (96%)
  local copies, waits for them, and re-layouts  1.28 us (4%)
    pallas_call x1, Pallas kernels, body(): pl.pallas_call(functools.partial(kernel, na, nb, nc), out_shape=jax.Shape...  33.4 us
    unnamed x1, local copies, waits for them, and re-layouts  1.28 us

profile of v2, /device:TPU:0, one launch (start us, length us, event | category | flops | bytes accessed | tf_op | source)
XLA Modules:
  0.0 34.7 jit_solution(14510611645778600257)
XLA Ops:
  0.0 33.4 %shard_map.37 = f32[8,128]{1,0:T(8,128)} custom-call(bf16[128,256]{1,0:T(8,128)(2,1)} %x_hbm.1, f32[8,128]{1,0:T(8,128)} %v_hbm.1, bf16[1,128]{1,0:T(2,128)(2,1)} %bitcast.1), custom_call_target="tpu_custom_call" | custom-call | tf_op jit(solution)/shard_map/pallas_call | solution.py:311
  33.4 1.3 %copy.5 = f32[8,128]{1,0:T(8,128)} copy(f32[8,128]{1,0:T(8,128)} %shard_map.37) | data formatting | bytes 8192

commit v3 on v2

--- a/solution.py
+++ b/solution.py
@@ -78,21 +78,9 @@
         kq, kp = slot // 2, slot % 2
         return member((q + kq) % nq, p if kp == 0 else 1 - p)
 
-    relay = nb == 4
     x_in, xc_in, v_in, db_in, da_in = {}, {}, {}, {}, {}
 
-    def to_line(step):
-        return pltpu.make_async_remote_copy(
-            src_ref=x_ref, dst_ref=xc.at[step], send_sem=xc_s.at[step],
-            recv_sem=xc_r.at[step], device_id=line(step), device_id_type=MESH,
-        )
-
-    order = [3, 1] if relay else list(range(1, nb))
-    if relay:
-        @pl.when(b % 3 == 0)
-        def _():
-            to_line(2).start()
-    for kb in order:
+    for kb in range(1, nb):
         xc_in[kb] = send(x_ref, xc.at[kb], xc_s.at[kb], xc_r.at[kb], line(kb))
     for kq in range(1, nq):
         slot = 2 * kq
@@ -167,16 +155,6 @@
         store_norm(kb, xj)
         unit(kb, 0, xj, xi, hi0)
 
-    if relay:
-        xc_in[1].wait_recv()
-        xc_in[3].wait_recv()
-
-        @pl.when(b % 3 != 0)
-        def _():
-            pltpu.make_async_remote_copy(
-                src_ref=xc.at[(5 - 2 * b) % 4], dst_ref=xc.at[2], send_sem=xc_s.at[2],
-                recv_sem=xc_r.at[2], device_id=line(2 * b - 3), device_id_type=MESH,
-            ).start()
     for kq in range(1, nq):
         pass_on(2 * kq)
     for kq in range(1, nq):
@@ -185,33 +163,20 @@
         v_in[slot + 1] = send(
             v0.at[slot], v0.at[slot + 1], v0_s.at[slot + 1], v0_r.at[slot + 1], partner
         )
-    if relay:
-        first(1)
-        first(3)
+    for kb in range(1, nb):
+        xc_in[kb].wait_recv()
+    others(first)
     his, pairs = [hi0], [xi]
     for kq in range(1, nq):
         x_in[2 * kq + 1].wait_recv()
         pairs.append(jnp.concatenate([xr[2 * kq], xr[2 * kq + 1]], axis=0))
         his.append(row_norm(pairs[kq]))
         unit(0, kq, own, pairs[kq], his[kq])
-        if relay:
-            unit(1, kq, xc[1], pairs[kq], his[kq])
-            unit(3, kq, xc[3], pairs[kq], his[kq])
-    if relay:
-        to_line(2).wait_recv()
-    else:
-        for kb in range(1, nb):
-            xc_in[kb].wait_recv()
-
-    def rest(kb):
-        first(kb)
-        for kq in range(1, nq):
+
+        def more(kb, kq=kq):
             unit(kb, kq, xc[kb], pairs[kq], his[kq])
 
-    if relay:
-        rest(2)
-    else:
-        others(rest)
+        others(more)
 
     for slot in range(1, na):
         if slot % 2:
@@ -285,8 +250,6 @@
     }
     for copy in pending[:-(na - 1)]:
         copy.wait_send()
-    if relay:
-        to_line(2).wait_send()
     for slot in range(1, na):
         mg_in[slot].wait_recv()
     every = jnp.sum(mg[...], axis=0)
@@ -310,7 +273,7 @@
         turns = (ITERS + 1) // 2
         return pl.pallas_call(
             functools.partial(kernel, na, nb, nc),
-            out_shape=jax.ShapeDtypeStruct((nk, span), F32),
+            out_shape=pltpu.VMEM((nk, span), F32),
             in_specs=[pl.BlockSpec(memory_space=pl.ANY)] * 3,
             out_specs=pl.BlockSpec(memory_space=pltpu.VMEM),
             scratch_shapes=[

time: 34.9 us -> 32.1 us (0.920)
  Pallas kernels: 33.4 us -> 31.4 us
  local copies, waits for them, and re-layouts: 1.28 us -> 0.6 us
    pallas_call x1, Pallas kernels: 33.4 us -> 31.4 us  [body(): pl.pallas_call(functools.partial(kernel, na, nb, nc), out_shape=pltpu.VME...]
    unnamed x1, local copies, waits for them, and re-layouts: 1.28 us -> 0.6 us
where the time goes in v3:
time: 32.1 us; the launch traced here: 32 us
  Pallas kernels  31.4 us (98%)
  local copies, waits for them, and re-layouts  0.6 us (2%)
    pallas_call x1, Pallas kernels, body(): pl.pallas_call(functools.partial(kernel, na, nb, nc), out_shape=pltpu.VME...  31.4 us

profile of v3, /device:TPU:0, one launch (start us, length us, event | category | flops | bytes accessed | tf_op | source)
XLA Modules:
  0.0 32.0 jit_solution(8318253722918354227)
XLA Ops:
  0.0 31.4 %shard_map.37 = f32[8,128]{1,0:T(8,128)S(1)} custom-call(bf16[128,256]{1,0:T(8,128)(2,1)} %x_hbm.1, f32[8,128]{1,0:T(8,128)} %v_hbm.1, bf16[1,128]{1,0:T(2,128)(2,1)} %bitcast.1), custom_call_target="tpu_custom_call" | custom-call | tf_op jit(solution)/shard_map/pallas_call | solution.py:274
  31.4 0.6 %copy.5 = f32[8,128]{1,0:T(8,128)} copy(f32[8,128]{1,0:T(8,128)S(1)} %shard_map.37) | data formatting | bytes 8192

commit v4 on v3

--- a/solution.py
+++ b/solution.py
@@ -163,9 +163,6 @@
         v_in[slot + 1] = send(
             v0.at[slot], v0.at[slot + 1], v0_s.at[slot + 1], v0_r.at[slot + 1], partner
         )
-    for kb in range(1, nb):
-        xc_in[kb].wait_recv()
-    others(first)
     his, pairs = [hi0], [xi]
     for kq in range(1, nq):
         x_in[2 * kq + 1].wait_recv()
@@ -173,10 +170,15 @@
         his.append(row_norm(pairs[kq]))
         unit(0, kq, own, pairs[kq], his[kq])
 
-        def more(kb, kq=kq):
+    for kb in range(1, nb):
+        xc_in[kb].wait_recv()
+
+    def rest(kb):
+        first(kb)
+        for kq in range(1, nq):
             unit(kb, kq, xc[kb], pairs[kq], his[kq])
 
-        others(more)
+    others(rest)
 
     for slot in range(1, na):
         if slot % 2:

time: 32.1 us -> 31.1 us (0.969)
  Pallas kernels: 31.4 us -> 30.3 us
    pallas_call x1, Pallas kernels: 31.4 us -> 30.3 us  [body(): pl.pallas_call(functools.partial(kernel, na, nb, nc), out_shape=pltpu.VME...]
where the time goes in v4:
time: 31.1 us; the launch traced here: 30.9 us
  Pallas kernels  30.3 us (97%)
  local copies, waits for them, and re-layouts  0.6 us (2%)
    pallas_call x1, Pallas kernels, body(): pl.pallas_call(functools.partial(kernel, na, nb, nc), out_shape=pltpu.VME...  30.3 us

profile of v4, /device:TPU:0, one launch (start us, length us, event | category | flops | bytes accessed | tf_op | source)
XLA Modules:
  0.0 30.9 jit_solution(12534471833941259393)
XLA Ops:
  0.0 30.3 %shard_map.37 = f32[8,128]{1,0:T(8,128)S(1)} custom-call(bf16[128,256]{1,0:T(8,128)(2,1)} %x_hbm.1, f32[8,128]{1,0:T(8,128)} %v_hbm.1, bf16[1,128]{1,0:T(2,128)(2,1)} %bitcast.1), custom_call_target="tpu_custom_call" | custom-call | tf_op jit(solution)/shard_map/pallas_call | solution.py:276
  30.3 0.6 %copy.5 = f32[8,128]{1,0:T(8,128)} copy(f32[8,128]{1,0:T(8,128)S(1)} %shard_map.37) | data formatting | bytes 8192
